TPU v7x, 32 devices: a whole 2x2x4 slice. The times are simulated.
32 devices in a mesh: fsdp: 2 (over x), ctx: 4 (over y, core), tp: 4 (over z).
Axes of the slice: x: 2, y: 2, z: 4, core: 2. Of those that a mesh axis runs over, the one named last changes fastest.
Arguments:
- hidden_in: bfloat16 [32, 512, 768], P('fsdp', 'ctx'), may hold values from -6 to 6
- lengths: int32 [32], P('fsdp'), may hold values from 128 to 512, as said below
- cotangent: bfloat16 [32, 512, 768], P('fsdp', 'ctx'), may hold values from -6 to 6
- w_qkv: bfloat16 [768, 3, 768], P(('fsdp', 'ctx'), None, 'tp'), may hold values from -0.21875 to 0.21875
- b_qv: bfloat16 [2, 768], P(None, 'tp'), may hold values from -1.5 to 1.5
- w_out: bfloat16 [768, 768], P('tp', ('fsdp', 'ctx')), may hold values from -2.5 to 2.5
- b_out: bfloat16 [768], P(('fsdp', 'ctx')), may hold values from -1.5 to 1.5
- gain_one: bfloat16 [768], P(('fsdp', 'ctx')), may hold values from 0.5 to 1.5
- shift_one: bfloat16 [768], P(('fsdp', 'ctx')), may hold values from -1.5 to 1.5
- w_in: bfloat16 [768, 3072], P(('fsdp', 'ctx'), 'tp'), may hold values from -0.21875 to 0.21875
- b_in: bfloat16 [3072], P('tp'), may hold values from -1.5 to 1.5
- w_down: bfloat16 [3072, 768], P('tp', ('fsdp', 'ctx')), may hold values from -0.109375 to 0.109375
- b_down: bfloat16 [768], P(('fsdp', 'ctx')), may hold values from -1.5 to 1.5
- gain_two: bfloat16 [768], P(('fsdp', 'ctx')), may hold values from 0.5 to 1.5
- shift_two: bfloat16 [768], P(('fsdp', 'ctx')), may hold values from -1.5 to 1.5
Outputs:
- hidden_out: bfloat16 [32, 512, 768], P('fsdp', 'ctx')
- grad_in: bfloat16 [32, 512, 768], P('fsdp', 'ctx')
- grad_w_qkv: float32 [768, 3, 768], P(('fsdp', 'ctx'), None, 'tp')
- grad_b_qv: float32 [2, 768], P(None, 'tp')
- grad_w_out: float32 [768, 768], P('tp', ('fsdp', 'ctx'))
- grad_b_out: float32 [768], P(('fsdp', 'ctx'))
- grad_gain_one: float32 [768], P(('fsdp', 'ctx'))
- grad_shift_one: float32 [768], P(('fsdp', 'ctx'))
- grad_w_in: float32 [768, 3072], P(('fsdp', 'ctx'), 'tp')
- grad_b_in: float32 [3072], P('tp')
- grad_w_down: float32 [3072, 768], P('tp', ('fsdp', 'ctx'))
- grad_b_down: float32 [768], P(('fsdp', 'ctx'))
- grad_gain_two: float32 [768], P(('fsdp', 'ctx'))
- grad_shift_two: float32 [768], P(('fsdp', 'ctx'))
Inputs may be any that keep to these rules, and one draw needn't show every extreme that they name: The first lengths[s] positions of slot s are valid, the rest padding; some slot has 512 and some 512 // 4.
All inputs are finite; a program needn't handle non-finite values.
Results may differ from a plain program's by a relative error of at most 0.015.
The roundings to bfloat16 on the way count: a program that leaves them out, or rounds other values in their place, can miss the bound.
Values may be sent and summed in bfloat16 or wider, within the bound.
A program may use at most 192 MiB of HBM per device.

v0:
```python
import jax
import jax.numpy as jnp
from jax import lax
from jax.sharding import PartitionSpec as P

HD = 64
SLOT_MB = 4
epsilon = 1e-05


def tp_total(partial_sum):
    return lax.psum(partial_sum, "tp")


def layer_norm(summed, gain_row, shift_row):
    center = summed - jnp.mean(summed, axis=-1, keepdims=True)
    inverse = lax.rsqrt(jnp.mean(center * center, axis=-1, keepdims=True) + epsilon)
    normed = center * inverse
    return (normed * gain_row + shift_row, normed, inverse)


def norm_back(incoming, normed, inverse, gain_row):
    scaled = incoming * gain_row
    result = inverse * (
        scaled
        - jnp.mean(scaled, axis=-1, keepdims=True)
        - normed * jnp.mean(scaled * normed, axis=-1, keepdims=True)
    )
    return (result, jnp.sum(incoming * normed, axis=0), jnp.sum(incoming, axis=0))


def attn_scores(queries, keys_all, key_valid, score_scale):
    raw_scores = (
        jnp.einsum("bqhe,bkhe->bhqk", queries, keys_all, preferred_element_type=jnp.float32)
        * score_scale
    )
    return jnp.where(key_valid[:, None, None, :], raw_scores, -1e30)


def on_device(
    hidden_in,
    lengths,
    cotangent,
    w_qkv,
    b_qv,
    w_out,
    b_out,
    gain_one,
    shift_one,
    w_in,
    b_in,
    w_down,
    b_down,
    gain_two,
    shift_two,
):
    local_slots, row_count, model_width = hidden_in.shape
    slot_batch = SLOT_MB
    micro_count = local_slots // slot_batch
    flat_rows = slot_batch * row_count
    key_count = row_count * lax.axis_size("ctx")
    local_width = w_qkv.shape[2]
    head_count = local_width // HD
    score_scale = HD ** (-0.5)
    row_place = lax.axis_index("ctx") * row_count + jnp.arange(row_count, dtype=jnp.int32)
    key_place = jnp.arange(key_count, dtype=jnp.int32)
    bias_three = jnp.stack([b_qv[0], jnp.zeros_like(b_qv[0]), b_qv[1]]).astype(jnp.float32)
    bias_in = b_in.astype(jnp.float32)
    bias_grads = (jnp.zeros((2, local_width), jnp.float32), jnp.zeros(b_in.shape, jnp.float32))
    outputs = []
    input_grads = []
    for micro_index in range(micro_count):
        gathered = (
            lax.all_gather(w_qkv, ("fsdp", "ctx"), axis=0, tiled=True),
            lax.all_gather(w_out, ("fsdp", "ctx"), axis=1, tiled=True),
            lax.all_gather(w_in, ("fsdp", "ctx"), axis=0, tiled=True),
            lax.all_gather(w_down, ("fsdp", "ctx"), axis=1, tiled=True),
            lax.all_gather(b_out, ("fsdp", "ctx"), axis=0, tiled=True),
            lax.all_gather(gain_one, ("fsdp", "ctx"), axis=0, tiled=True),
            lax.all_gather(shift_one, ("fsdp", "ctx"), axis=0, tiled=True),
            lax.all_gather(b_down, ("fsdp", "ctx"), axis=0, tiled=True),
            lax.all_gather(gain_two, ("fsdp", "ctx"), axis=0, tiled=True),
            lax.all_gather(shift_two, ("fsdp", "ctx"), axis=0, tiled=True),
        )
        full_qkv, full_out, full_in, full_down = (
            gathered[0],
            gathered[1],
            gathered[2],
            gathered[3],
        )
        full_bout = gathered[4].astype(jnp.float32)
        full_gain_one = gathered[5].astype(jnp.float32)
        full_shift_one = gathered[6].astype(jnp.float32)
        full_bdown = gathered[7].astype(jnp.float32)
        full_gain_two = gathered[8].astype(jnp.float32)
        full_shift_two = gathered[9].astype(jnp.float32)
        first_slot = micro_index * slot_batch
        tokens = hidden_in[first_slot : first_slot + slot_batch].reshape(flat_rows, model_width)
        length = lengths[first_slot : first_slot + slot_batch]
        row_valid = (row_place[None, :] < length[:, None]).astype(jnp.float32).reshape(flat_rows)
        key_valid = key_place[None, :] < length[:, None]
        qkv_local = (
            jnp.einsum("sd,dcf->scf", tokens, full_qkv, preferred_element_type=jnp.float32)
            + bias_three
        ).astype(jnp.bfloat16)
        kv_local = qkv_local[:, 1:].reshape(slot_batch, row_count, 2, local_width)
        key_value = lax.all_gather(kv_local, "ctx", axis=1, tiled=True)
        queries = qkv_local[:, 0].reshape(slot_batch, row_count, head_count, HD)
        keys_all = key_value[:, :, 0].reshape(slot_batch, key_count, head_count, HD)
        values_all = key_value[:, :, 1].reshape(slot_batch, key_count, head_count, HD)
        scores = attn_scores(queries, keys_all, key_valid, score_scale)
        highest = jnp.max(scores, axis=-1, keepdims=True)
        exponent = jnp.exp(scores - highest)
        denominator = jnp.sum(exponent, axis=-1, keepdims=True)
        log_total = highest + jnp.log(denominator)
        probs_low = (exponent / denominator).astype(jnp.bfloat16)
        context = (
            jnp.einsum("bhqk,bkhe->bqhe", probs_low, values_all, preferred_element_type=jnp.float32)
            .astype(jnp.bfloat16)
            .reshape(flat_rows, local_width)
        )
        attended = (
            tp_total(jnp.dot(context, full_out, preferred_element_type=jnp.float32)) + full_bout
        )
        first_out, normed_one, inverse_one = layer_norm(
            tokens.astype(jnp.float32) + attended, full_gain_one, full_shift_one
        )
        first_low = first_out.astype(jnp.bfloat16)
        pre_act = jnp.dot(first_low, full_in, preferred_element_type=jnp.float32) + bias_in
        activated = jax.nn.gelu(pre_act, approximate=False).astype(jnp.bfloat16)
        branch = (
            tp_total(jnp.dot(activated, full_down, preferred_element_type=jnp.float32)) + full_bdown
        )
        result, normed_two, inverse_two = layer_norm(
            first_out + branch, full_gain_two, full_shift_two
        )
        outputs.append(result.astype(jnp.bfloat16).reshape(slot_batch, row_count, model_width))
        incoming = (
            cotangent[first_slot : first_slot + slot_batch]
            .reshape(flat_rows, model_width)
            .astype(jnp.float32)
            * row_valid[:, None]
        )
        grad_two, grad_gain_two, grad_shift_two = norm_back(
            incoming, normed_two, inverse_two, full_gain_two
        )
        grad_branch = grad_two.astype(jnp.bfloat16)
        grad_bdown = jnp.sum(grad_branch.astype(jnp.float32), axis=0)
        grad_wdown = jnp.einsum(
            "sf,sd->fd", activated, grad_branch, preferred_element_type=jnp.float32
        )
        grad_act = jnp.einsum(
            "sd,fd->sf", grad_branch, full_down, preferred_element_type=jnp.float32
        )
        _, gelu_back = jax.vjp(
            lambda inner_value: jax.nn.gelu(inner_value, approximate=False), pre_act
        )
        grad_pre = gelu_back(grad_act)[0].astype(jnp.bfloat16)
        grad_win = jnp.einsum("sd,sf->df", first_low, grad_pre, preferred_element_type=jnp.float32)
        grad_bin = jnp.sum(grad_pre.astype(jnp.float32), axis=0)
        grad_first = grad_two + tp_total(
            jnp.einsum("sf,df->sd", grad_pre, full_in, preferred_element_type=jnp.float32)
        )
        grad_one, grad_gain_one, grad_shift_one = norm_back(
            grad_first, normed_one, inverse_one, full_gain_one
        )
        grad_attended = grad_one.astype(jnp.bfloat16)
        grad_bout = jnp.sum(grad_attended.astype(jnp.float32), axis=0)
        grad_wout = jnp.einsum(
            "sf,sd->fd", context, grad_attended, preferred_element_type=jnp.float32
        )
        grad_context = (
            jnp.einsum("sd,fd->sf", grad_attended, full_out, preferred_element_type=jnp.float32)
            .astype(jnp.bfloat16)
            .reshape(slot_batch, row_count, head_count, HD)
        )
        scores_again = attn_scores(queries, keys_all, key_valid, score_scale)
        weights_back = jnp.exp(scores_again - log_total)
        grad_probs = jnp.einsum(
            "bqhe,bkhe->bhqk", grad_context, values_all, preferred_element_type=jnp.float32
        )
        grad_scores = (
            weights_back * (grad_probs - jnp.sum(grad_probs * weights_back, axis=-1, keepdims=True))
        ).astype(jnp.bfloat16)
        grad_query = (
            jnp.einsum("bhqk,bkhe->bqhe", grad_scores, keys_all, preferred_element_type=jnp.float32)
            * score_scale
        )
        grad_key = (
            jnp.einsum("bhqk,bqhe->bkhe", grad_scores, queries, preferred_element_type=jnp.float32)
            * score_scale
        )
        grad_value = jnp.einsum(
            "bhqk,bqhe->bkhe",
            weights_back.astype(jnp.bfloat16),
            grad_context,
            preferred_element_type=jnp.float32,
        )
        key_value_terms = jnp.stack(
            [
                grad_key.reshape(slot_batch, key_count, local_width),
                grad_value.reshape(slot_batch, key_count, local_width),
            ],
            axis=2,
        )
        key_value_grad = lax.psum_scatter(key_value_terms, "ctx", scatter_dimension=1, tiled=True)
        grad_qkv = (
            jnp.concatenate(
                [grad_query.reshape(slot_batch, row_count, 1, local_width), key_value_grad], axis=2
            )
            .astype(jnp.bfloat16)
            .reshape(flat_rows, 3, local_width)
        )
        grad_wqkv = jnp.einsum("sd,scf->dcf", tokens, grad_qkv, preferred_element_type=jnp.float32)
        qkv_sums = jnp.sum(grad_qkv.astype(jnp.float32), axis=0)
        grad_bqv = jnp.stack([qkv_sums[0], qkv_sums[2]])
        grad_tokens = grad_one + tp_total(
            jnp.einsum("scf,dcf->sd", grad_qkv, full_qkv, preferred_element_type=jnp.float32)
        )
        input_grads.append(
            grad_tokens.astype(jnp.bfloat16).reshape(slot_batch, row_count, model_width)
        )
        bias_grads = (bias_grads[0] + grad_bqv, bias_grads[1] + grad_bin)
        pieces = (
            lax.psum_scatter(grad_wqkv, ("fsdp", "ctx"), scatter_dimension=0, tiled=True),
            lax.psum_scatter(grad_wout, ("fsdp", "ctx"), scatter_dimension=1, tiled=True),
            lax.psum_scatter(grad_win, ("fsdp", "ctx"), scatter_dimension=0, tiled=True),
            lax.psum_scatter(grad_wdown, ("fsdp", "ctx"), scatter_dimension=1, tiled=True),
            lax.psum_scatter(grad_bout, ("fsdp", "ctx"), scatter_dimension=0, tiled=True),
            lax.psum_scatter(grad_gain_one, ("fsdp", "ctx"), scatter_dimension=0, tiled=True),
            lax.psum_scatter(grad_shift_one, ("fsdp", "ctx"), scatter_dimension=0, tiled=True),
            lax.psum_scatter(grad_bdown, ("fsdp", "ctx"), scatter_dimension=0, tiled=True),
            lax.psum_scatter(grad_gain_two, ("fsdp", "ctx"), scatter_dimension=0, tiled=True),
            lax.psum_scatter(grad_shift_two, ("fsdp", "ctx"), scatter_dimension=0, tiled=True),
        )
        grad_shards = pieces if micro_index == 0 else jax.tree.map(jnp.add, grad_shards, pieces)
    bias_total = lax.psum((bias_grads[0], bias_grads[1]), ("fsdp", "ctx"))
    return (
        jnp.concatenate(outputs, axis=0),
        jnp.concatenate(input_grads, axis=0),
        grad_shards[0],
        bias_total[0],
        grad_shards[1],
        grad_shards[4],
        grad_shards[5],
        grad_shards[6],
        grad_shards[2],
        bias_total[1],
        grad_shards[3],
        grad_shards[7],
        grad_shards[8],
        grad_shards[9],
    )


def solution(mesh):
    return jax.shard_map(
        on_device,
        mesh=mesh,
        in_specs=(
            P("fsdp", "ctx", None),
            P("fsdp"),
            P("fsdp", "ctx", None),
            P(("fsdp", "ctx"), None, "tp"),
            P(None, "tp"),
            P("tp", ("fsdp", "ctx")),
            P(("fsdp", "ctx")),
            P(("fsdp", "ctx")),
            P(("fsdp", "ctx")),
            P(("fsdp", "ctx"), "tp"),
            P("tp"),
            P("tp", ("fsdp", "ctx")),
            P(("fsdp", "ctx")),
            P(("fsdp", "ctx")),
            P(("fsdp", "ctx")),
        ),
        out_specs=(
            P("fsdp", "ctx", None),
            P("fsdp", "ctx", None),
            P(("fsdp", "ctx"), None, "tp"),
            P(None, "tp"),
            P("tp", ("fsdp", "ctx")),
            P(("fsdp", "ctx")),
            P(("fsdp", "ctx")),
            P(("fsdp", "ctx")),
            P(("fsdp", "ctx"), "tp"),
            P("tp"),
            P("tp", ("fsdp", "ctx")),
            P(("fsdp", "ctx")),
            P(("fsdp", "ctx")),
            P(("fsdp", "ctx")),
        ),
        check_vma=False,
    )
```

profile of v0, /device:TPU:0, one launch (start us, length us, event | category | flops | bytes accessed | tf_op | source)
XLA Modules:
  0.0 1470.3 jit_solution(5045254554735531446)
XLA Ops:
  8.1 3.0 fusion.200
  11.2 15.5 %all_gather.28 = bf16[768,3,192]{2,1,0:T(4,128)(2,1)} all-gather(bf16[96,3,192]{2,1,0:T(4,128)(2,1)S(1)} %copy.105), channel_id=1, replica_groups=mesh['fsdp'=2,'ctx'=4,'tp'=4] {'fsdp','ctx'}, dimensions={0}, use_global_device_ids=true | all-gather | bytes 995328 | tf_op jit(solution)/shard_map/all_gather | solution.py:74
  26.7 2.6 copy.106
  38.8 9.6 all_gather.30
  51.6 4.2 all-gather.17.cloned.1.call-done
  58.0 19.4 %all-gather.15.cloned.1.call-done = bf16[4,512,2,192]{1,0,3,2:T(4,128)(2,1)} async-done(((bf16[4,128,2,192]{1,0,3,2:T(4,128)(2,1)}), bf16[4,512,2,192]{1,0,3,2:T(4,128)(2,1)}) %all-gather.15.cloned.1.call-update) | async-done | bytes 1572880 | tf_op jit(solution)/shard_map/all_gather | solution.py:107
  88.4 10.5 all-gather.13.cloned.1.call-done
  110.2 9.9 all-gather.7.cloned.1.call-done
  136.2 25.5 %all-reduce.17 = (bf16[768]{0:T(1024)(128)(2,1)}, bf16[768]{0:T(1024)(128)(2,1)}, bf16[768]{0:T(1024)(128)(2,1)}, bf16[768]{0:T(1024)(128)(2,1)}, bf16[768]{0:T(1024)(128)(2,1)}, /*index=5*/bf16[768]{0:T(1024)(128)(2,1)}) all-reduce(bf16[768]{0:T(1024)(128)(2,1)S(1)} %dynamic-update-slice, ...), channel_id=1, replica_groups=mesh['fsdp'=2,'ctx'=4,'tp'=4] {'fsdp','ctx'}, use_global_device_ids=true, to_apply=%add | all-reduce | flops 4608 | bytes 18432
  163.7 187.5 %all-reduce.29.cloned.1.call-done = (f32[512,768]{1,0:T(8,128)}, f32[512,768]{1,0:T(8,128)}, f32[512,768]{1,0:T(8,128)}, f32[512,768]{1,0:T(8,128)}) async-done(((f32[512,768]{1,0:T(8,128)}, f32[512,768]{1,0:T(8,128)}, f32[512,768]{1,0:T(8,128)}, f32[512,768]{1,0:T(8,128)}), (f32[512,768]{1,0:T(8,128)}, f32[512,768]{1,0:T(8,128)}, f32[512,768]{1,0:T(8,128)}, ...) | async-done | bytes 6291472 | tf_op jit(solution)/shard_map/psum | solution.py:12
  351.3 4.6 fusion.193
  360.4 7.9 multiply_convert_fusion.4
  368.3 5.7 multiply_convert_fusion.5
  374.0 3.6 fusion.223
  377.6 2.0 fusion.221
  379.6 5.5 multiply_convert_fusion.6
  385.1 2.0 fusion.219
  387.1 5.8 multiply_convert_fusion.7
  393.8 2.0 fusion.217
  400.3 3.8 multiply_reduce_fusion.23
  405.3 212.5 %all-reduce.27.cloned.1.call-done = (f32[512,768]{1,0:T(8,128)}, f32[512,768]{1,0:T(8,128)}, f32[512,768]{1,0:T(8,128)}, f32[512,768]{1,0:T(8,128)}) async-done(((f32[512,768]{1,0:T(8,128)}, f32[512,768]{1,0:T(8,128)}, f32[512,768]{1,0:T(8,128)}, f32[512,768]{1,0:T(8,128)}), (f32[512,768]{1,0:T(8,128)}, f32[512,768]{1,0:T(8,128)}, f32[512,768]{1,0:T(8,128)}, ...) | async-done | bytes 6291472 | tf_op jit(solution)/shard_map/psum | solution.py:12
  617.8 2.6 fusion.191
  622.0 3.1 fusion.188
  627.0 2.7 multiply_reduce_fusion.4
  631.7 3.1 convert_reduce_fusion.2
  634.8 3.1 convert_reduce_fusion.3
  640.5 2.1 fusion.227
  645.0 2.0 fusion.226
  649.6 2.0 fusion.225
  654.9 2.0 fusion.224
  657.7 221.2 %all-reduce.25.cloned.1.call-done = (f32[512,768]{1,0:T(8,128)}, f32[512,768]{1,0:T(8,128)}, f32[512,768]{1,0:T(8,128)}, f32[512,768]{1,0:T(8,128)}) async-done(((f32[512,768]{1,0:T(8,128)}, f32[512,768]{1,0:T(8,128)}, f32[512,768]{1,0:T(8,128)}, f32[512,768]{1,0:T(8,128)}), (f32[512,768]{1,0:T(8,128)}, f32[512,768]{1,0:T(8,128)}, f32[512,768]{1,0:T(8,128)}, ...) | async-done | bytes 6291472 | tf_op jit(solution)/shard_map/psum | solution.py:12
  879.0 5.5 multiply_reduce_fusion.11
  885.9 3.8 convert_reduce_fusion.11
  889.7 3.8 convert_reduce_fusion.10
  897.5 3.4 multiply_reduce_fusion.1
  903.7 2.0 pad_maximum_fusion.3
  906.5 2.5 convolution_convert_fusion.2
  910.6 4.0 multiply_reduce_fusion.2
  917.6 1.9 pad_maximum_fusion.2
  920.3 2.5 convolution_convert_fusion.3
  924.5 2.3 multiply_reduce_fusion.3
  929.6 1.9 pad_maximum_fusion.1
  932.7 2.5 convolution_convert_fusion
  936.2 2.2 multiply_reduce_fusion
  941.2 2.0 pad_maximum_fusion.4
  957.7 2.8 fusion.73
  960.5 22.3 %reduce-scatter.15.cloned.1.call-done = f32[4,128,2,192]{1,3,0,2:T(8,128)} async-done(((f32[4,512,2,192]{1,3,0,2:T(8,128)}), f32[4,128,2,192]{1,3,0,2:T(8,128)}) %reduce-scatter.15.cloned.1.call-update) | async-done | bytes 786448 | tf_op jit(solution)/shard_map/reduce_scatter | solution.py:206
  982.8 2.0 convert.55
  984.8 38.1 %reduce-scatter.13.cloned.1.call-done = f32[4,128,2,192]{1,3,0,2:T(8,128)} async-done(((f32[4,512,2,192]{1,3,0,2:T(8,128)}), f32[4,128,2,192]{1,3,0,2:T(8,128)}) %reduce-scatter.13.cloned.1.call-update) | async-done | bytes 786448 | tf_op jit(solution)/shard_map/reduce_scatter | solution.py:206
  1022.9 2.0 convert.53
  1024.9 38.9 %reduce-scatter.19.cloned.1.call-done = f32[4,128,2,192]{1,3,0,2:T(8,128)} async-done(((f32[4,512,2,192]{1,3,0,2:T(8,128)}), f32[4,128,2,192]{1,3,0,2:T(8,128)}) %reduce-scatter.19.cloned.1.call-update) | async-done | bytes 786448 | tf_op jit(solution)/shard_map/reduce_scatter | solution.py:206
  1070.0 2.8 copy.160
  1075.9 2.0 convolution_bitcast_fusion
  1078.0 2.0 convolution_bitcast_fusion.1
  1080.0 2.0 convolution_bitcast_fusion.2
  1082.9 2.0 convolution_bitcast_fusion.3
  1086.3 2.2 fusion.179
  1091.8 2.5 add_add_fusion.1
  1100.9 2.3 add_add_fusion
  1112.1 23.7 %all-reduce.12 = (f32[2,192]{1,0:T(2,128)}, f32[768]{0:T(1024)S(1)}, f32[768]{0:T(1024)S(1)}, f32[768]{0:T(1024)S(1)}, f32[768]{0:T(1024)}, /*index=5*/f32[768]{0:T(1024)S(1)}, f32[768]{0:T(1024)S(1)}, f32[768]{0:T(1024)S(1)}) all-reduce(f32[2,192]{1,0:T(2,128)S(1)} %fusion.133, ...), channel_id=1, replica_groups=mesh['fsdp'=2,'ctx'=4,'tp'=4] {'fsdp','ctx'}, use_global_device_ids=true, to_apply=%region_72.73 | all-reduce | flops 5760 | bytes 46080 | tf_op jit(solution)/shard_map/psum | solution.py:237
  1139.3 6.7 reduce-scatter.25.cloned.1.call-done
  1148.0 223.4 %all-reduce.23.cloned.1.call-done = (f32[512,768]{1,0:T(8,128)}, f32[512,768]{1,0:T(8,128)}, f32[512,768]{1,0:T(8,128)}, f32[512,768]{1,0:T(8,128)}) async-done(((f32[512,768]{1,0:T(8,128)}, f32[512,768]{1,0:T(8,128)}, f32[512,768]{1,0:T(8,128)}, f32[512,768]{1,0:T(8,128)}), (f32[512,768]{1,0:T(8,128)}, f32[512,768]{1,0:T(8,128)}, f32[512,768]{1,0:T(8,128)}, ...) | async-done | bytes 6291472 | tf_op jit(solution)/shard_map/psum | solution.py:12
  1379.7 36.8 %reduce-scatter.21.cloned.1.call-done = f32[96,768]{1,0:T(8,128)} async-done(((f32[768,768]{1,0:T(8,128)}), f32[96,768]{1,0:T(8,128)}) %reduce-scatter.21.cloned.1.call-update) | async-done | bytes 294928 | tf_op jit(solution)/shard_map/reduce_scatter | solution.py:227
  1416.5 46.2 %reduce-scatter.23.cloned.1.call-done = f32[768,96]{0,1:T(8,128)} async-done(((f32[768,768]{0,1:T(8,128)}), f32[768,96]{0,1:T(8,128)}) %reduce-scatter.23.cloned.1.call-update) | async-done | bytes 294928 | tf_op jit(solution)/shard_map/reduce_scatter | solution.py:228
  (727 shorter events, 162.7 us)
Async XLA Ops:
  8.0 47.8 %all-gather.17.cloned.1.call-start = ((), (), s32[]{:S(2)}) async-start(), calls=%async_computation.13 | async-start | bytes 1966080 | tf_op jit(solution)/shard_map/all_gather | solution.py:107
  11.0 18.3 %copy-start.55 = (bf16[4,128,768]{2,1,0:T(8,128)(2,1)}, bf16[4,128,768]{2,1,0:T(8,128)(2,1)S(1)}, u32[]{:S(2)}) copy-start(bf16[4,128,768]{2,1,0:T(8,128)(2,1)S(1)} %get-tuple-element.170) | copy-start | bytes 2359300
  11.0 19.0 %copy-start.56 = (bf16[4,128,768]{2,1,0:T(8,128)(2,1)}, bf16[4,128,768]{2,1,0:T(8,128)(2,1)S(1)}, u32[]{:S(2)}) copy-start(bf16[4,128,768]{2,1,0:T(8,128)(2,1)S(1)} %get-tuple-element.171) | copy-start | bytes 2359300
  11.1 20.7 %copy-start.57 = (bf16[4,128,768]{2,1,0:T(8,128)(2,1)}, bf16[4,128,768]{2,1,0:T(8,128)(2,1)S(1)}, u32[]{:S(2)}) copy-start(bf16[4,128,768]{2,1,0:T(8,128)(2,1)S(1)} %get-tuple-element.172) | copy-start | bytes 2359300
  34.7 42.7 %all-gather.15.cloned.1.call-start = ((), (), s32[]{:S(2)}) async-start(), calls=%async_computation.12 | async-start | bytes 1966080 | tf_op jit(solution)/shard_map/all_gather | solution.py:107
  35.7 63.2 %all-gather.13.cloned.1.call-start = ((), (), s32[]{:S(2)}) async-start(), calls=%async_computation.11 | async-start | bytes 1966080 | tf_op jit(solution)/shard_map/all_gather | solution.py:107
  36.6 83.5 %all-gather.7.cloned.1.call-start = ((), (), s32[]{:S(2)}) async-start(), calls=%async_computation.8 | async-start | bytes 1966080 | tf_op jit(solution)/shard_map/all_gather | solution.py:107
  37.6 11.6 copy-start.202
  37.6 313.7 %all-reduce.29.cloned.1.call-start = ((), (), s32[]{:S(2)}) async-start(), calls=%async_computation.25 | async-start | bytes 12582912 | tf_op jit(solution)/shard_map/psum | solution.py:12
  57.8 24.1 %copy-start.72 = (bf16[4,512,1,192]{1,3,0,2:T(8,128)(2,1)}, bf16[4,512,1,192]{1,3,0,2:T(8,128)(2,1)S(1)}, u32[]{:S(2)}) copy-start(bf16[4,512,1,192]{1,3,0,2:T(8,128)(2,1)S(1)} %copy.123) | copy-start | bytes 2359300
  58.0 21.7 %copy-start.59 = (bf16[4,512,1,192]{1,3,0,2:T(8,128)(2,1)}, bf16[4,512,1,192]{1,3,0,2:T(8,128)(2,1)S(1)}, u32[]{:S(2)}) copy-start(bf16[4,512,1,192]{1,3,0,2:T(8,128)(2,1)S(1)} %copy.124) | copy-start | bytes 2359300
  79.5 6.6 copy-start.75
  79.6 4.7 copy-start.61
  88.2 17.3 %copy-start.89 = (bf16[4,128,3,64]{1,0,3,2:T(4,128)(2,1)}, bf16[4,128,3,64]{1,0,3,2:T(4,128)(2,1)S(1)}, u32[]{:S(2)}) copy-start(bf16[4,128,3,64]{1,0,3,2:T(4,128)(2,1)S(1)} %copy.126) | copy-start | bytes 589828
  88.3 18.7 %copy-start.91 = (bf16[4,128,3,64]{1,0,3,2:T(4,128)(2,1)}, bf16[4,128,3,64]{1,0,3,2:T(4,128)(2,1)S(1)}, u32[]{:S(2)}) copy-start(bf16[4,128,3,64]{1,0,3,2:T(4,128)(2,1)S(1)} %copy.121) | copy-start | bytes 589828
  128.2 232.1 %all-gather.9.cloned.1.call-start = ((), (), s32[]{:S(2)}) async-start(), calls=%async_computation.9 | async-start | bytes 1327104 | tf_op jit(solution)/shard_map/all_gather | solution.py:76
  128.8 245.2 %all-gather.11.cloned.1.call-start = ((), (), s32[]{:S(2)}) async-start(), calls=%async_computation.10 | async-start | bytes 1327104 | tf_op jit(solution)/shard_map/all_gather | solution.py:77
  129.4 488.4 %all-reduce.27.cloned.1.call-start = ((), (), s32[]{:S(2)}) async-start(), calls=%async_computation.24 | async-start | bytes 12582912 | tf_op jit(solution)/shard_map/psum | solution.py:12
  163.1 457.7 %copy-start.130 = (f32[768]{0:T(1024)}, f32[768]{0:T(1024)S(1)}, u32[]{:S(2)}) copy-start(f32[768]{0:T(1024)S(1)} %convert_element_type.382) | copy-start | bytes 9220
  356.2 4.1 copy-start.132
  360.3 7.9 copy-start.10
  360.3 7.9 copy-start.141
  360.3 7.9 copy-start.157
  360.3 7.9 copy-start.211
  360.3 7.9 copy-start.217
  374.0 3.6 copy-start.117
  374.0 3.6 copy-start.220
  395.8 483.1 %all-reduce.25.cloned.1.call-start = ((), (), s32[]{:S(2)}) async-start(), calls=%async_computation.23 | async-start | bytes 12582912 | tf_op jit(solution)/shard_map/psum | solution.py:12
  634.8 12.3 copy-start.50
  634.8 3.9 copy-start.236
  637.9 4.7 copy-start.36
  637.9 13.7 copy-start.52
  657.0 299.4 %reduce-scatter.17.cloned.1.call-start = ((), (), s32[]{:S(2)}) async-start(), calls=%async_computation.16 | async-start | bytes 3932160 | tf_op jit(solution)/shard_map/reduce_scatter | solution.py:206
  878.9 5.6 copy-start.7
  878.9 5.6 copy-start.12
  878.9 5.6 copy-start.22
  878.9 5.6 copy-start.37
  878.9 6.1 copy-start.48
  878.9 6.5 copy-start.104
  878.9 6.9 copy-start.105
  878.9 6.9 copy-start.133
  878.9 6.9 copy-start.143
  879.0 6.9 copy-start.148
  879.0 6.9 copy-start.159
  879.0 6.9 copy-start.163
  885.9 3.8 copy-start.17
  885.9 3.8 copy-start.138
  885.9 3.8 copy-start.155
  905.7 77.1 %reduce-scatter.15.cloned.1.call-start = ((), (), s32[]{:S(2)}) async-start(), calls=%async_computation.15 | async-start | bytes 3932160 | tf_op jit(solution)/shard_map/reduce_scatter | solution.py:206
  910.6 4.0 copy-start.3
  919.5 103.4 %reduce-scatter.13.cloned.1.call-start = ((), (), s32[]{:S(2)}) async-start(), calls=%async_computation.14 | async-start | bytes 3932160 | tf_op jit(solution)/shard_map/reduce_scatter | solution.py:206
  931.6 4.6 copy-start.1
  931.6 132.2 %reduce-scatter.19.cloned.1.call-start = ((), (), s32[]{:S(2)}) async-start(), calls=%async_computation.17 | async-start | bytes 3932160 | tf_op jit(solution)/shard_map/reduce_scatter | solution.py:206
  943.3 164.0 %reduce-scatter.27.cloned.1.call-start = ((), (), s32[]{:S(2)}) async-start(), calls=%async_computation.21 | async-start | bytes 884736
  956.3 189.8 %reduce-scatter.25.cloned.1.call-start = ((), (), s32[]{:S(2)}) async-start(), calls=%async_computation.20 | async-start | bytes 2211840
  1072.8 298.6 %all-reduce.23.cloned.1.call-start = ((), (), s32[]{:S(2)}) async-start(), calls=%async_computation.22 | async-start | bytes 12582912 | tf_op jit(solution)/shard_map/psum | solution.py:12
  1085.0 3.6 copy-start.23
  1085.0 3.6 copy-start.149
  1085.0 3.6 copy-start.164
  1085.0 331.5 %reduce-scatter.21.cloned.1.call-start = ((), (), s32[]{:S(2)}) async-start(), calls=%async_computation.18 | async-start | bytes 2654208 | tf_op jit(solution)/shard_map/reduce_scatter | solution.py:227
  1094.4 368.3 %reduce-scatter.23.cloned.1.call-start = ((), (), s32[]{:S(2)}) async-start(), calls=%async_computation.19 | async-start | bytes 2654208 | tf_op jit(solution)/shard_map/reduce_scatter | solution.py:228
  1106.9 4.7 copy-start.113
  1106.9 4.9 copy-start.115
  1110.2 261.3 %copy-start.33 = (f32[512,768]{1,0:T(8,128)S(1)}, f32[512,768]{1,0:T(8,128)}, u32[]{:S(2)}) copy-start(f32[512,768]{1,0:T(8,128)} %get-tuple-element.214) | copy-start | bytes 4718596
  (191 other events, 343.8 us)
Sparse Core Ops, SparseCore 0:
  34.8 20.9 all-gather.16
  57.3 20.0 all-gather.14
  79.0 19.8 all-gather.12
  100.3 19.8 all-gather.6
  128.3 222.9 all-reduce.28
  396.0 221.7 all-reduce.26
  657.1 221.7 all-reduce.24
  905.8 36.6 reduce-scatter.16
  945.0 37.7 reduce-scatter.14
  985.2 37.7 reduce-scatter.12
  1026.0 37.7 reduce-scatter.18
  1066.8 34.9 reduce-scatter.26
  1105.7 40.3 reduce-scatter.24
  1148.5 222.8 all-reduce.22
  1375.2 41.2 reduce-scatter.20
  1420.3 42.3 reduce-scatter.22
Sparse Core Ops, SparseCore 1:
  130.6 24.0 all-gather.8
  156.4 23.8 all-gather.10
where the time goes:
time: 1480 us; the launch traced here: 1470 us
  waiting for transfers between devices  1080 us (73%)
  matrix products  123 us (8%)
  local copies, waits for them, and re-layouts  88.7 us (6%)
  other arithmetic  83.5 us (6%)
  blocking collectives  74.4 us (5%)
  between operations  20 us (1%)
    psum x4, waiting for transfers between devices, tp_total(): return lax.psum(partial_sum, 'tp')  845 us
    reduce_scatter x4, waiting for transfers between devices, on_device(): lax.psum_scatter(key_value_terms, 'ctx', scatter_dimension=1, tiled=True)  99.3 us
    unnamed x504, local copies, waits for them, and re-layouts  59.3 us
    reduce_scatter x1, waiting for transfers between devices, on_device(): lax.psum_scatter(grad_wdown, ('fsdp', 'ctx'), scatter_dimension=1, tiled=...  46.2 us
    all_gather x4, waiting for transfers between devices, on_device(): key_value = lax.all_gather(kv_local, 'ctx', axis=1, tiled=True)  44 us
    reduce_scatter x1, waiting for transfers between devices, on_device(): lax.psum_scatter(grad_win, ('fsdp', 'ctx'), scatter_dimension=0, tiled=True)  36.8 us
  transfers between devices with their start and end apart: 18, of which 14 were waited for; matrix products, arithmetic and copies ran while one was open for 11% of the time, Pallas kernels for 0%

commit v1 on v0

--- a/solution.py
+++ b/solution.py
@@ -2,6 +2,7 @@
 import jax.numpy as jnp
 from jax import lax
 from jax.sharding import PartitionSpec as P
+from jax.lax import axis_index, axis_size, ppermute
 
 HD = 64
 SLOT_MB = 4
@@ -104,7 +105,17 @@
             + bias_three
         ).astype(jnp.bfloat16)
         kv_local = qkv_local[:, 1:].reshape(slot_batch, row_count, 2, local_width)
-        key_value = lax.all_gather(kv_local, "ctx", axis=1, tiled=True)
+        step_out = axis_size("ctx")
+        mid_arr = axis_index("ctx")
+        w_next, u1 = (step_out, mid_arr)
+        key_value, arr_next = (kv_local, 1)
+        while arr_next < w_next:
+            e_next = tuple(((h, h ^ arr_next) for h in range(w_next)))
+            answer = ppermute(key_value, axis_name="ctx", perm=e_next)
+            state_now = jnp.concatenate([key_value, answer], 1)
+            all_values = jnp.concatenate([answer, key_value], 1)
+            key_value = jnp.where(u1 & arr_next == 0, state_now, all_values)
+            arr_next = 2 * arr_next
         queries = qkv_local[:, 0].reshape(slot_batch, row_count, head_count, HD)
         keys_all = key_value[:, :, 0].reshape(slot_batch, key_count, head_count, HD)
         values_all = key_value[:, :, 1].reshape(slot_batch, key_count, head_count, HD)

time: 1480 us -> 1330 us (0.90)
  waiting for transfers between devices: 1080 us -> 900 us
  blocking collectives: 74.4 us -> 93.5 us
  other arithmetic: 83.5 us -> 98.5 us
    psum x4, waiting for transfers between devices: 845 us -> 774 us  [tp_total(): return lax.psum(partial_sum, 'tp')]
    reduce_scatter x1, waiting for transfers between devices: 46.2 us -> 0.01 us  [on_device(): lax.psum_scatter(grad_wdown, ('fsdp', 'ctx'), scatter_dimension=1, tiled=...]
    all_gather x4 -> x0, waiting for transfers between devices: 44 us -> none  [on_device(): key_value = lax.all_gather(kv_local, 'ctx', axis=1, tiled=True)]
    reduce_scatter x1, waiting for transfers between devices: 36.8 us -> 0.01 us  [on_device(): lax.psum_scatter(grad_win, ('fsdp', 'ctx'), scatter_dimension=0, tiled=True)]
    ppermute x0 -> x8, waiting for transfers between devices: none -> 20.4 us  [on_device(): answer = ppermute(key_value, axis_name='ctx', perm=e_next)]
    unnamed x504 -> x508, local copies, waits for them, and re-layouts: 59.3 us -> 59.4 us
  transfers between devices with their start and end apart: 18 -> 22, of which waited for: 14 -> 11; matrix products, arithmetic and copies ran while one was open for 11% -> 13% of each run, Pallas kernels for 0% -> 0%
where the time goes in v1:
time: 1330 us; the launch traced here: 1320 us
  waiting for transfers between devices  900 us (68%)
  matrix products  123 us (9%)
  other arithmetic  98.5 us (7%)
  blocking collectives  93.5 us (7%)
  local copies, waits for them, and re-layouts  80 us (6%)
  between operations  20.1 us (2%)
    psum x4, waiting for transfers between devices, tp_total(): return lax.psum(partial_sum, 'tp')  774 us
    reduce_scatter x4, waiting for transfers between devices, on_device(): lax.psum_scatter(key_value_terms, 'ctx', scatter_dimension=1, tiled=True)  99.2 us
    unnamed x508, local copies, waits for them, and re-layouts  59.4 us
    unnamed x1, blocking collectives  33.1 us
  transfers between devices with their start and end apart: 22, of which 11 were waited for; matrix products, arithmetic and copies ran while one was open for 13% of the time, Pallas kernels for 0%

profile of v1, /device:TPU:0, one launch (start us, length us, event | category | flops | bytes accessed | tf_op | source)
XLA Modules:
  0.0 1321.5 jit_solution(7072063190319602990)
XLA Ops:
  8.1 3.0 fusion.200
  11.2 15.5 %all_gather.20 = bf16[768,3,192]{2,1,0:T(4,128)(2,1)} all-gather(bf16[96,3,192]{2,1,0:T(4,128)(2,1)S(1)} %copy.105), channel_id=1, replica_groups=mesh['fsdp'=2,'ctx'=4,'tp'=4] {'fsdp','ctx'}, dimensions={0}, use_global_device_ids=true | all-gather | bytes 995328 | tf_op jit(solution)/shard_map/all_gather | solution.py:75
  26.7 2.6 copy.106
  42.0 20.1 %all_gather.21 = bf16[192,768]{0,1:T(8,128)(2,1)S(1)} all-gather(bf16[192,96]{0,1:T(8,128)(2,1)S(1)} %copy.111), channel_id=1, replica_groups=mesh['fsdp'=2,'ctx'=4,'tp'=4] {'fsdp','ctx'}, dimensions={1}, use_global_device_ids=true | all-gather | bytes 331776 | tf_op jit(solution)/shard_map/all_gather | solution.py:76
  65.3 2.2 maximum_select_fusion.5
  68.3 2.2 maximum_select_fusion.4
  72.0 2.9 maximum_select_fusion.3
  79.9 4.5 collective-permute-done.5
  90.5 10.6 collective-permute-done.3
  112.1 5.3 collective-permute-done.1
  133.5 33.1 %all-reduce.17 = (bf16[768]{0:T(1024)(128)(2,1)}, bf16[768]{0:T(1024)(128)(2,1)}, bf16[768]{0:T(1024)(128)(2,1)}, bf16[768]{0:T(1024)(128)(2,1)}, bf16[768]{0:T(1024)(128)(2,1)}, /*index=5*/bf16[768]{0:T(1024)(128)(2,1)}) all-reduce(bf16[768]{0:T(1024)(128)(2,1)S(1)} %dynamic-update-slice, ...), channel_id=1, replica_groups=mesh['fsdp'=2,'ctx'=4,'tp'=4] {'fsdp','ctx'}, use_global_device_ids=true, to_apply=%add | all-reduce | flops 4608 | bytes 18432
  168.6 180.3 %all-reduce.29.cloned.1.call-done = (f32[512,768]{1,0:T(8,128)}, f32[512,768]{1,0:T(8,128)}, f32[512,768]{1,0:T(8,128)}, f32[512,768]{1,0:T(8,128)}) async-done(((f32[512,768]{1,0:T(8,128)}, f32[512,768]{1,0:T(8,128)}, f32[512,768]{1,0:T(8,128)}, f32[512,768]{1,0:T(8,128)}), (f32[512,768]{1,0:T(8,128)}, f32[512,768]{1,0:T(8,128)}, f32[512,768]{1,0:T(8,128)}, ...) | async-done | bytes 6291472 | tf_op jit(solution)/shard_map/psum | solution.py:13
  348.8 4.6 fusion.193
  358.2 7.8 multiply_convert_fusion.4
  366.1 5.7 multiply_convert_fusion.5
  371.7 3.6 fusion.223
  375.4 2.0 fusion.221
  377.4 5.5 multiply_convert_fusion.6
  382.9 2.0 fusion.219
  384.9 5.8 multiply_convert_fusion.7
  391.7 2.0 fusion.217
  398.2 3.8 multiply_reduce_fusion.23
  403.2 212.4 %all-reduce.27.cloned.1.call-done = (f32[512,768]{1,0:T(8,128)}, f32[512,768]{1,0:T(8,128)}, f32[512,768]{1,0:T(8,128)}, f32[512,768]{1,0:T(8,128)}) async-done(((f32[512,768]{1,0:T(8,128)}, f32[512,768]{1,0:T(8,128)}, f32[512,768]{1,0:T(8,128)}, f32[512,768]{1,0:T(8,128)}), (f32[512,768]{1,0:T(8,128)}, f32[512,768]{1,0:T(8,128)}, f32[512,768]{1,0:T(8,128)}, ...) | async-done | bytes 6291472 | tf_op jit(solution)/shard_map/psum | solution.py:13
  615.6 2.6 fusion.191
  619.9 3.1 fusion.188
  624.9 2.7 multiply_reduce_fusion.4
  629.5 3.1 convert_reduce_fusion.2
  632.7 3.1 convert_reduce_fusion.3
  638.4 2.1 fusion.227
  642.9 2.0 fusion.226
  647.4 2.0 fusion.225
  652.8 2.0 fusion.224
  655.6 221.2 %all-reduce.25.cloned.1.call-done = (f32[512,768]{1,0:T(8,128)}, f32[512,768]{1,0:T(8,128)}, f32[512,768]{1,0:T(8,128)}, f32[512,768]{1,0:T(8,128)}) async-done(((f32[512,768]{1,0:T(8,128)}, f32[512,768]{1,0:T(8,128)}, f32[512,768]{1,0:T(8,128)}, f32[512,768]{1,0:T(8,128)}), (f32[512,768]{1,0:T(8,128)}, f32[512,768]{1,0:T(8,128)}, f32[512,768]{1,0:T(8,128)}, ...) | async-done | bytes 6291472 | tf_op jit(solution)/shard_map/psum | solution.py:13
  876.9 5.5 multiply_reduce_fusion.11
  883.8 3.8 convert_reduce_fusion.11
  887.7 3.8 convert_reduce_fusion.10
  895.4 3.4 multiply_reduce_fusion.1
  901.6 2.0 pad_maximum_fusion.3
  904.3 2.5 convolution_convert_fusion.2
  908.5 4.1 multiply_reduce_fusion.2
  915.5 1.9 pad_maximum_fusion.2
  918.2 2.5 convolution_convert_fusion.3
  922.4 2.3 multiply_reduce_fusion.3
  927.5 1.9 pad_maximum_fusion.1
  930.6 2.5 convolution_convert_fusion
  934.1 2.2 multiply_reduce_fusion
  939.1 2.0 pad_maximum_fusion.4
  955.5 2.8 fusion.73
  958.2 22.1 %reduce-scatter.15.cloned.1.call-done = f32[4,128,2,192]{1,3,0,2:T(8,128)} async-done(((f32[4,512,2,192]{1,3,0,2:T(8,128)}), f32[4,128,2,192]{1,3,0,2:T(8,128)}) %reduce-scatter.15.cloned.1.call-update) | async-done | bytes 786448 | tf_op jit(solution)/shard_map/reduce_scatter | solution.py:217
  980.4 2.0 convert.55
  982.3 38.3 %reduce-scatter.13.cloned.1.call-done = f32[4,128,2,192]{1,3,0,2:T(8,128)} async-done(((f32[4,512,2,192]{1,3,0,2:T(8,128)}), f32[4,128,2,192]{1,3,0,2:T(8,128)}) %reduce-scatter.13.cloned.1.call-update) | async-done | bytes 786448 | tf_op jit(solution)/shard_map/reduce_scatter | solution.py:217
  1020.6 2.0 convert.53
  1022.6 38.8 %reduce-scatter.19.cloned.1.call-done = f32[4,128,2,192]{1,3,0,2:T(8,128)} async-done(((f32[4,512,2,192]{1,3,0,2:T(8,128)}), f32[4,128,2,192]{1,3,0,2:T(8,128)}) %reduce-scatter.19.cloned.1.call-update) | async-done | bytes 786448 | tf_op jit(solution)/shard_map/reduce_scatter | solution.py:217
  1067.6 2.8 copy.160
  1073.6 2.0 convolution_bitcast_fusion
  1075.6 2.0 convolution_bitcast_fusion.1
  1077.7 2.0 convolution_bitcast_fusion.2
  1080.6 2.0 convolution_bitcast_fusion.3
  1084.0 2.2 fusion.179
  1090.2 2.5 add_add_fusion.1
  1099.2 2.4 add_add_fusion
  1110.4 24.8 %all-reduce.12 = (f32[2,192]{1,0:T(2,128)}, f32[768]{0:T(1024)S(1)}, f32[768]{0:T(1024)S(1)}, f32[768]{0:T(1024)S(1)}, f32[768]{0:T(1024)}, /*index=5*/f32[768]{0:T(1024)S(1)}, f32[768]{0:T(1024)S(1)}, f32[768]{0:T(1024)S(1)}) all-reduce(f32[2,192]{1,0:T(2,128)S(1)} %fusion.133, ...), channel_id=1, replica_groups=mesh['fsdp'=2,'ctx'=4,'tp'=4] {'fsdp','ctx'}, use_global_device_ids=true, to_apply=%region_72.73 | all-reduce | flops 5760 | bytes 46080 | tf_op jit(solution)/shard_map/psum | solution.py:248
  1138.7 4.7 reduce-scatter.25.cloned.1.call-done
  1145.4 160.2 %all-reduce.23.cloned.1.call-done = (f32[512,768]{1,0:T(8,128)}, f32[512,768]{1,0:T(8,128)}, f32[512,768]{1,0:T(8,128)}, f32[512,768]{1,0:T(8,128)}) async-done(((f32[512,768]{1,0:T(8,128)}, f32[512,768]{1,0:T(8,128)}, f32[512,768]{1,0:T(8,128)}, f32[512,768]{1,0:T(8,128)}), (f32[512,768]{1,0:T(8,128)}, f32[512,768]{1,0:T(8,128)}, f32[512,768]{1,0:T(8,128)}, ...) | async-done | bytes 6291472 | tf_op jit(solution)/shard_map/psum | solution.py:13
  (743 shorter events, 166.5 us)
Async XLA Ops:
  8.0 340.8 %all-reduce.29.cloned.1.call-start = ((), (), s32[]{:S(2)}) async-start(), calls=%async_computation.21 | async-start | bytes 12582912 | tf_op jit(solution)/shard_map/psum | solution.py:13
  11.0 18.3 %copy-start.55 = (bf16[4,128,768]{2,1,0:T(8,128)(2,1)}, bf16[4,128,768]{2,1,0:T(8,128)(2,1)S(1)}, u32[]{:S(2)}) copy-start(bf16[4,128,768]{2,1,0:T(8,128)(2,1)S(1)} %get-tuple-element.170) | copy-start | bytes 2359300
  11.0 19.0 %copy-start.56 = (bf16[4,128,768]{2,1,0:T(8,128)(2,1)}, bf16[4,128,768]{2,1,0:T(8,128)(2,1)S(1)}, u32[]{:S(2)}) copy-start(bf16[4,128,768]{2,1,0:T(8,128)(2,1)S(1)} %get-tuple-element.171) | copy-start | bytes 2359300
  11.1 20.7 %copy-start.57 = (bf16[4,128,768]{2,1,0:T(8,128)(2,1)}, bf16[4,128,768]{2,1,0:T(8,128)(2,1)S(1)}, u32[]{:S(2)}) copy-start(bf16[4,128,768]{2,1,0:T(8,128)(2,1)S(1)} %get-tuple-element.172) | copy-start | bytes 2359300
  33.9 2.5 collective-permute-start.6
  34.5 27.6 %collective-permute-start.4 = (bf16[4,128,2,192]{1,0,3,2:T(4,128)(2,1)S(1)}, bf16[4,128,2,192]{1,0,3,2:T(4,128)(2,1)}, u32[]{:S(2)}, u32[]{:S(2)}) collective-permute-start(bf16[4,128,2,192]{1,0,3,2:T(4,128)(2,1)S(1)} %reshape.611), channel_id=1, source_target_pairs={{0,4},{4,0},{8,12},{12,8},{1,5},{5,1},{9,13},{13,9},{2,6},{6,2},{1... | collective-permute-start | bytes 1179656 | tf_op jit(solution)/shard_map/ppermute | solution.py:114
  34.9 30.5 %collective-permute-start.2 = (bf16[4,128,2,192]{1,0,3,2:T(4,128)(2,1)S(1)}, bf16[4,128,2,192]{1,0,3,2:T(4,128)(2,1)}, u32[]{:S(2)}, u32[]{:S(2)}) collective-permute-start(bf16[4,128,2,192]{1,0,3,2:T(4,128)(2,1)S(1)} %reshape.607), channel_id=1, source_target_pairs={{0,4},{4,0},{8,12},{12,8},{1,5},{5,1},{9,13},{13,9},{2,6},{6,2},{1... | collective-permute-start | bytes 1179656 | tf_op jit(solution)/shard_map/ppermute | solution.py:114
  36.2 32.1 %collective-permute-start = (bf16[4,128,2,192]{1,0,3,2:T(4,128)(2,1)}, bf16[4,128,2,192]{1,0,3,2:T(4,128)(2,1)}, u32[]{:S(2)}, u32[]{:S(2)}) collective-permute-start(bf16[4,128,2,192]{1,0,3,2:T(4,128)(2,1)} %reshape.603), channel_id=1, source_target_pairs={{0,4},{4,0},{8,12},{12,8},{1,5},{5,1},{9,13},{13,9},{2,6},{6,2},{1... | collective-permute-start | bytes 1179656 | tf_op jit(solution)/shard_map/ppermute | solution.py:114
  36.4 4.5 copy-start.205
  36.4 4.5 copy-start.206
  36.4 4.5 copy-start.207
  36.4 4.6 copy-start.208
  36.4 4.6 copy-start.152
  38.2 33.8 %collective-permute-start.7 = (bf16[4,256,2,192]{1,0,3,2:T(4,128)(2,1)S(1)}, bf16[4,256,2,192]{1,0,3,2:T(4,128)(2,1)}, u32[]{:S(2)}, u32[]{:S(2)}) collective-permute-start(bf16[4,256,2,192]{1,0,3,2:T(4,128)(2,1)S(1)} %maximum_select_fusion.7), channel_id=1, source_target_pairs={{0,8},{4,12},{8,0},{12,4},{1,9},{5,13},{9,1},{13,5},{2,10},{6,14},... | collective-permute-start | bytes 2359304 | tf_op jit(solution)/shard_map/ppermute | solution.py:114
  41.2 34.6 %copy-start.82 = (bf16[4,128,3,64]{1,0,3,2:T(4,128)(2,1)}, bf16[4,128,3,64]{1,0,3,2:T(4,128)(2,1)S(1)}, u32[]{:S(2)}) copy-start(bf16[4,128,3,64]{1,0,3,2:T(4,128)(2,1)S(1)} %reshape_squeeze.46) | copy-start | bytes 589828
  41.2 45.2 %copy-start.88 = (bf16[4,128,3,64]{1,0,3,2:T(4,128)(2,1)}, bf16[4,128,3,64]{1,0,3,2:T(4,128)(2,1)S(1)}, u32[]{:S(2)}) copy-start(bf16[4,128,3,64]{1,0,3,2:T(4,128)(2,1)S(1)} %reshape_squeeze.43) | copy-start | bytes 589828
  41.3 62.0 %copy-start.86 = (bf16[4,128,3,64]{1,0,3,2:T(4,128)(2,1)}, bf16[4,128,3,64]{1,0,3,2:T(4,128)(2,1)S(1)}, u32[]{:S(2)}) copy-start(bf16[4,128,3,64]{1,0,3,2:T(4,128)(2,1)S(1)} %reshape_squeeze.40) | copy-start | bytes 589828
  63.8 20.5 %collective-permute-start.5 = (bf16[4,256,2,192]{1,0,3,2:T(4,128)(2,1)S(1)}, bf16[4,256,2,192]{1,0,3,2:T(4,128)(2,1)S(1)}, u32[]{:S(2)}, u32[]{:S(2)}) collective-permute-start(bf16[4,256,2,192]{1,0,3,2:T(4,128)(2,1)S(1)} %maximum_select_fusion.6), channel_id=1, source_target_pairs={{0,8},{4,12},{8,0},{12,4},{1,9},{5,13},{9,1},{13,5},{2,10},{6,14},... | collective-permute-start | bytes 2359304 | tf_op jit(solution)/shard_map/ppermute | solution.py:114
  67.6 33.6 %collective-permute-start.3 = (bf16[4,256,2,192]{1,0,3,2:T(4,128)(2,1)S(1)}, bf16[4,256,2,192]{1,0,3,2:T(4,128)(2,1)S(1)}, u32[]{:S(2)}, u32[]{:S(2)}) collective-permute-start(bf16[4,256,2,192]{1,0,3,2:T(4,128)(2,1)S(1)} %maximum_select_fusion.5), channel_id=1, source_target_pairs={{0,8},{4,12},{8,0},{12,4},{1,9},{5,13},{9,1},{13,5},{2,10},{6,14},... | collective-permute-start | bytes 2359304 | tf_op jit(solution)/shard_map/ppermute | solution.py:114
  70.5 46.9 %collective-permute-start.1 = (bf16[4,256,2,192]{1,0,3,2:T(4,128)(2,1)S(1)}, bf16[4,256,2,192]{1,0,3,2:T(4,128)(2,1)S(1)}, u32[]{:S(2)}, u32[]{:S(2)}) collective-permute-start(bf16[4,256,2,192]{1,0,3,2:T(4,128)(2,1)S(1)} %maximum_select_fusion.4), channel_id=1, source_target_pairs={{0,8},{4,12},{8,0},{12,4},{1,9},{5,13},{9,1},{13,5},{2,10},{6,14},... | collective-permute-start | bytes 2359304 | tf_op jit(solution)/shard_map/ppermute | solution.py:114
  79.8 27.5 %copy-start.90 = (bf16[4,128,3,64]{1,0,3,2:T(4,128)(2,1)}, bf16[4,128,3,64]{1,0,3,2:T(4,128)(2,1)S(1)}, u32[]{:S(2)}) copy-start(bf16[4,128,3,64]{1,0,3,2:T(4,128)(2,1)S(1)} %copy.126) | copy-start | bytes 589828
  90.5 18.4 %copy-start.92 = (bf16[4,128,3,64]{1,0,3,2:T(4,128)(2,1)}, bf16[4,128,3,64]{1,0,3,2:T(4,128)(2,1)S(1)}, u32[]{:S(2)}) copy-start(bf16[4,128,3,64]{1,0,3,2:T(4,128)(2,1)S(1)} %copy.121) | copy-start | bytes 589828
  125.5 232.7 %all-gather.3.cloned.1.call-start = ((), (), s32[]{:S(2)}) async-start(), calls=%async_computation.8 | async-start | bytes 1327104 | tf_op jit(solution)/shard_map/all_gather | solution.py:77
  126.1 245.7 %all-gather.5.cloned.1.call-start = ((), (), s32[]{:S(2)}) async-start(), calls=%async_computation.9 | async-start | bytes 1327104 | tf_op jit(solution)/shard_map/all_gather | solution.py:78
  126.7 489.0 %all-reduce.27.cloned.1.call-start = ((), (), s32[]{:S(2)}) async-start(), calls=%async_computation.20 | async-start | bytes 12582912 | tf_op jit(solution)/shard_map/psum | solution.py:13
  167.9 450.7 %copy-start.132 = (f32[768]{0:T(1024)}, f32[768]{0:T(1024)S(1)}, u32[]{:S(2)}) copy-start(f32[768]{0:T(1024)S(1)} %convert_element_type.382) | copy-start | bytes 9220
  353.8 4.4 copy-start.134
  358.2 7.9 copy-start.10
  358.2 7.9 copy-start.143
  358.2 7.9 copy-start.159
  358.2 7.9 copy-start.213
  358.2 7.9 copy-start.219
  393.7 483.1 %all-reduce.25.cloned.1.call-start = ((), (), s32[]{:S(2)}) async-start(), calls=%async_computation.19 | async-start | bytes 12582912 | tf_op jit(solution)/shard_map/psum | solution.py:13
  632.6 12.3 copy-start.50
  632.7 3.9 copy-start.238
  635.7 4.7 copy-start.36
  635.7 13.7 %copy-start.52 = (f32[512,768]{1,0:T(8,128)}, f32[512,768]{1,0:T(8,128)S(1)}, u32[]{:S(2)}) copy-start(f32[512,768]{1,0:T(8,128)S(1)} %get-tuple-element.125) | copy-start | bytes 4718596
  654.9 299.2 %reduce-scatter.17.cloned.1.call-start = ((), (), s32[]{:S(2)}) async-start(), calls=%async_computation.12 | async-start | bytes 3932160 | tf_op jit(solution)/shard_map/reduce_scatter | solution.py:217
  876.8 5.6 copy-start.7
  876.8 5.6 copy-start.12
  876.8 5.6 copy-start.22
  876.8 5.6 copy-start.37
  876.8 6.1 copy-start.48
  876.8 6.5 copy-start.105
  876.8 6.9 copy-start.106
  876.8 6.9 copy-start.135
  876.8 6.9 copy-start.145
  876.9 6.9 copy-start.150
  876.9 6.9 copy-start.161
  876.9 6.9 copy-start.165
  883.8 3.8 copy-start.17
  903.6 76.8 %reduce-scatter.15.cloned.1.call-start = ((), (), s32[]{:S(2)}) async-start(), calls=%async_computation.11 | async-start | bytes 3932160 | tf_op jit(solution)/shard_map/reduce_scatter | solution.py:217
  908.5 4.1 copy-start.3
  917.5 103.1 %reduce-scatter.13.cloned.1.call-start = ((), (), s32[]{:S(2)}) async-start(), calls=%async_computation.10 | async-start | bytes 3932160 | tf_op jit(solution)/shard_map/reduce_scatter | solution.py:217
  929.4 4.7 copy-start.1
  929.5 131.9 %reduce-scatter.19.cloned.1.call-start = ((), (), s32[]{:S(2)}) async-start(), calls=%async_computation.13 | async-start | bytes 3932160 | tf_op jit(solution)/shard_map/reduce_scatter | solution.py:217
  941.1 164.5 %reduce-scatter.27.cloned.1.call-start = ((), (), s32[]{:S(2)}) async-start(), calls=%async_computation.17 | async-start | bytes 884736
  954.0 189.5 %reduce-scatter.25.cloned.1.call-start = ((), (), s32[]{:S(2)}) async-start(), calls=%async_computation.16 | async-start | bytes 2211840
  1070.5 235.2 %all-reduce.23.cloned.1.call-start = ((), (), s32[]{:S(2)}) async-start(), calls=%async_computation.18 | async-start | bytes 12582912 | tf_op jit(solution)/shard_map/psum | solution.py:13
  1082.6 231.2 %reduce-scatter.21.cloned.1.call-start = ((), (), s32[]{:S(2)}) async-start(), calls=%async_computation.14 | async-start | bytes 2654208 | tf_op jit(solution)/shard_map/reduce_scatter | solution.py:238
  1092.7 221.1 %reduce-scatter.23.cloned.1.call-start = ((), (), s32[]{:S(2)}) async-start(), calls=%async_computation.15 | async-start | bytes 2654208 | tf_op jit(solution)/shard_map/reduce_scatter | solution.py:239
  1105.3 4.7 copy-start.115
  1105.3 4.8 copy-start.117
  1108.6 197.1 %copy-start.33 = (f32[512,768]{1,0:T(8,128)S(1)}, f32[512,768]{1,0:T(8,128)}, u32[]{:S(2)}) copy-start(f32[512,768]{1,0:T(8,128)} %get-tuple-element.214) | copy-start | bytes 4718596
  (197 other events, 366.5 us)
Sparse Core Ops, SparseCore 0:
  125.6 223.1 all-reduce.28
  393.8 221.7 all-reduce.26
  655.0 221.7 all-reduce.24
  1082.7 222.8 all-reduce.22
Sparse Core Ops, SparseCore 1:
  127.9 24.2 all-gather.2
  153.8 23.9 all-gather.4
  903.6 36.5 reduce-scatter.16
  942.8 37.5 reduce-scatter.14
  982.9 37.6 reduce-scatter.12
  1023.7 37.6 reduce-scatter.18
  1064.4 34.9 reduce-scatter.26
  1103.2 40.2 reduce-scatter.24
  1147.3 42.2 reduce-scatter.20
  1193.4 42.2 reduce-scatter.22
